TPU v7x, 32 devices: a 4x2x2 block of a 4x4x8 slice. The times are simulated.
32 devices in a mesh: dp: 4 (over y, z), dcp: 8 (over x, core).
Axes of the slice: x: 4, y: 2, z: 2, core: 2. Of those that a mesh axis runs over, the one named last changes fastest.
The devices are a block of a 4x4x8 slice.
Arguments:
- q_abs: bfloat16 [128, 128, 576], P('dp', 'dcp'), parts along dimension 0
- cache: bfloat16 [128, 8192, 576], P('dp', 'dcp'), parts along dimension 0
- lengths: int32 [128], P('dp'), parts along dimension 0
Outputs:
- output: bfloat16 [128, 128, 512], P('dp', 'dcp'), parts along dimension 0
There are 4 independent parts. A program takes and returns all parts, laid end to end along the dimension named above; each array names one.
All inputs are finite; a program needn't handle non-finite values.
Results may differ from a plain program's by a relative error of at most 0.00716151.
Values are sent between devices in bfloat16 or wider.
A program may use at most 768 MiB of HBM per device.

v0:
```python
import jax
import jax.numpy as jnp
from jax import lax
from jax.sharding import PartitionSpec as P

ROPE = 64
SCALE = 192 ** -0.5


def partial_attention(q, blk, valid, lat):
    s = jnp.einsum('bhk,btk->bht', q, blk, preferred_element_type=jnp.float32) * SCALE
    s = jnp.where(valid[:, None, :], s, -jnp.inf)
    m = jnp.max(s, axis=2)
    m0 = jnp.where(jnp.isfinite(m), m, 0.0)
    p = jnp.exp(s - m0[:, :, None])
    l = jnp.sum(p, axis=2)
    pv = jnp.einsum('bht,btc->bhc', p.astype(jnp.bfloat16), blk[:, :, :lat], preferred_element_type=jnp.float32)
    has = l > 0.0
    l1 = jnp.where(has, l, 1.0)
    od = (pv / l1[:, :, None]).astype(jnp.bfloat16)
    lse = jnp.where(has, m0 + jnp.log(l1), -jnp.inf)
    return od, lse


def merge(od, lse, axis):
    mx = jnp.max(lse, axis=axis, keepdims=True)
    wt = jnp.exp(lse - mx)
    wt = wt / jnp.sum(wt, axis=axis, keepdims=True)
    return jnp.sum(wt[..., None] * od.astype(jnp.float32), axis=axis).astype(jnp.bfloat16)


def solution(mesh):
    n = mesh.shape['dcp']

    def local(q, cache, lengths):
        d = lax.axis_index('dcp')
        b, sl, wd = cache.shape
        lat = wd - ROPE
        qa = lax.all_gather(q, 'dcp', axis=1, tiled=True)
        pos = d * sl + jnp.arange(sl)
        valid = pos[None, :] < lengths[:, None]
        od, lse = partial_attention(qa, cache, valid, lat)
        h = od.shape[1]
        od = od.reshape(b, n, h // n, lat)
        lse = lse.reshape(b, n, h // n)
        od = lax.all_to_all(od, 'dcp', 1, 1, tiled=True)
        lse = lax.all_to_all(lse, 'dcp', 1, 1, tiled=True)
        return merge(od, lse, 1)

    return jax.shard_map(local, mesh=mesh, in_specs=(P('dp', 'dcp', None), P('dp', 'dcp', None), P('dp')), out_specs=P('dp', 'dcp', None), check_vma=False)
```

profile of v0, /device:TPU:88, one launch (start us, length us, event | category | flops | bytes accessed | tf_op | source)
XLA Modules:
  0.0 164.0 jit_solution(619272856210306433)
XLA Ops:
  6.5 0.0 all-gather.2.cloned.1.call-start
  6.6 0.7 all-gather.2.cloned.1.call-update
  7.3 0.7 broadcast_compare_fusion
  8.1 36.7 %all-gather.2.cloned.1.call-done = bf16[32,128,576]{2,1,0:T(8,128)(2,1)} async-done(((bf16[32,16,576]{2,1,0:T(8,128)(2,1)}), bf16[32,128,576]{2,1,0:T(8,128)(2,1)}) %all-gather.2.cloned.1.call-update) | async-done | bytes 4718608 | tf_op jit(solution)/shard_map/all_gather | solution.py:39
  44.8 20.5 %fusion.2 = (f32[32,128]{1,0:T(8,128)S(1)}, f32[32,128,1024]{2,1,0:T(8,128)}) fusion(pred[32,1024]{1,0:T(8,128)(4,1)S(1)} %broadcast_compare_fusion, bf16[32,128,576]{2,1,0:T(8,128)(2,1)} %all-gather.2.cloned.1.call-done, bf16[32,1024,576]{1,2,0:T(8,128)(2,1)} %param.4), kind=kOutput, calls=%fused_computation.4 | convolution fusion | flops 4844417024 | bytes 59293696 | tf_op jit(solution)/shard_map/bhk,btk->bht/dot_general | solution.py:11
  65.3 0.1 copy.10
  65.4 8.0 %fusion.4 = f32[32,128]{1,0:T(8,128)S(1)} fusion(f32[32,128,1024]{2,1,0:T(8,128)} %get-tuple-element.6, f32[32,128]{1,0:T(8,128)S(1)} %is-finite_select_fusion.1, pred[32,1024]{1,0:T(8,128)(4,1)S(1)} %broadcast_compare_fusion), kind=kLoop, calls=%fused_computation.6 | loop fusion | flops 16773120 | bytes 16842752 | tf_op jit(solution)/shard_map/reduce_sum | solution.py:16
  73.4 0.1 copy.9
  73.6 0.7 reshape.45
  74.3 3.5 %all-to-all-start = ((f32[8,1,512]{2,1,0:T(1,128)}), f32[8,1,512]{2,1,0:T(1,128)S(1)}, u32[]{:S(2)}, u32[]{:S(2)}) async-start(f32[8,1,512]{2,1,0:T(1,128)} %reshape.45), calls=%async_computation | async-start | bytes 32768 | tf_op jit(solution)/shard_map/all_to_all | solution.py:47
  77.8 19.0 %divide_convert_fusion = bf16[32,128,512]{2,1,0:T(8,128)(2,1)S(1)} fusion(f32[32,128]{1,0:T(8,128)S(1)} %compare_select_fusion.2, bf16[32,1024,576]{1,2,0:T(8,128)(2,1)} %param.4, f32[32,128,1024]{2,1,0:T(8,128)} %get-tuple-element.6, f32[32,128]{1,0:T(8,128)S(1)} %is-finite_select_fusion.1, pred[32,1024]{1,0:T(8,128)(4,1)S(1)} %broadcast_compare_fusion), kind=kOutput, calls=%fused_computation.8 | convolution fusion | flops 4315938816 | bytes 54591488 | tf_op jit(solution)/shard_map/bht,btc->bhc/dot_general | solution.py:17
  96.8 2.4 %copy.13 = bf16[32,8,16,512]{3,2,0,1:T(8,128)(2,1)} copy(bf16[32,8,16,512]{3,2,1,0:T(8,128)(2,1)S(1)} %bitcast.11) | data formatting | bytes 8388608 | tf_op jit(solution)/shard_map/reshape | solution.py:44
  99.3 0.0 all-to-all-done
  99.3 4.7 %all-to-all-start.1 = ((bf16[32,8,16,512]{3,2,0,1:T(8,128)(2,1)}), bf16[32,8,16,512]{3,2,0,1:T(8,128)(2,1)}, u32[]{:S(2)}, u32[]{:S(2)}) async-start(bf16[32,8,16,512]{3,2,0,1:T(8,128)(2,1)} %copy.13), calls=%async_computation.1 | async-start | bytes 8388608 | tf_op jit(solution)/shard_map/all_to_all | solution.py:46
  104.0 0.5 broadcast.38
  104.5 0.7 reduce
  105.2 0.1 reshape.46
  105.4 0.1 copy.11
  105.5 48.0 %all-to-all-done.1 = bf16[32,8,16,512]{3,2,0,1:T(8,128)(2,1)} async-done(((bf16[32,8,16,512]{3,2,0,1:T(8,128)(2,1)}), bf16[32,8,16,512]{3,2,0,1:T(8,128)(2,1)}, u32[]{:S(2)}, u32[]{:S(2)}) %all-to-all-start.1) | async-done | bytes 4194336 | tf_op jit(solution)/shard_map/all_to_all | solution.py:46
  153.5 3.6 %multiply_reduce_fusion = bf16[32,16,512]{2,1,0:T(8,128)(2,1)} fusion(bf16[32,8,16,512]{3,2,0,1:T(8,128)(2,1)} %all-to-all-done.1, f32[32,8,16]{2,0,1:T(8,128)S(1)} %copy.11), kind=kLoop, calls=%fused_computation.7 | loop fusion | flops 6029312 | bytes 4734976 | tf_op jit(solution)/shard_map/reduce_sum | solution.py:29
  (7 shorter events, 0.1 us)
Async XLA Ops:
  6.5 38.2 %all-gather.2.cloned.1.call-start = ((), (), s32[]{:S(2)}) async-start(), calls=%async_computation.2 | async-start | bytes 5898240 | tf_op jit(solution)/shard_map/all_gather | solution.py:39
  74.3 25.0 %all-to-all-start = ((f32[8,1,512]{2,1,0:T(1,128)}), f32[8,1,512]{2,1,0:T(1,128)S(1)}, u32[]{:S(2)}, u32[]{:S(2)}) async-start(f32[8,1,512]{2,1,0:T(1,128)} %reshape.45), calls=%async_computation | async-start | bytes 32768 | tf_op jit(solution)/shard_map/all_to_all | solution.py:47
  99.3 54.2 %all-to-all-start.1 = ((bf16[32,8,16,512]{3,2,0,1:T(8,128)(2,1)}), bf16[32,8,16,512]{3,2,0,1:T(8,128)(2,1)}, u32[]{:S(2)}, u32[]{:S(2)}) async-start(bf16[32,8,16,512]{3,2,0,1:T(8,128)(2,1)} %copy.13), calls=%async_computation.1 | async-start | bytes 8388608 | tf_op jit(solution)/shard_map/all_to_all | solution.py:46
Sparse Core Ops, SparseCore 0:
  8.9 35.7 all-gather.1
where the time goes:
time: 165 us; the launch traced here: 164 us
  waiting for transfers between devices  85.5 us (52%)
  matrix products  39.5 us (24%)
  between operations  13.5 us (8%)
  other arithmetic  13.2 us (8%)
  starting transfers between devices  8.27 us (5%)
  local copies, waits for them, and re-layouts  4.01 us (2%)
    all_to_all x1, waiting for transfers between devices, local(): od = lax.all_to_all(od, 'dcp', 1, 1, tiled=True)  48 us
    all_gather x1, waiting for transfers between devices, local(): qa = lax.all_gather(q, 'dcp', axis=1, tiled=True)  36.7 us
    dot_general x1, matrix products, partial_attention(): jnp.einsum('bhk,btk->bht', q, blk, preferred_element_type=jnp.float32)  20.5 us
    dot_general x1, matrix products, partial_attention(): jnp.einsum('bht,btc->bhc', p.astype(jnp.bfloat16), blk[:, :, :lat], prefe...  19 us
    reduce_sum x1, other arithmetic, partial_attention(): l = jnp.sum(p, axis=2)  8.03 us
    all_to_all x1, starting transfers between devices, local(): od = lax.all_to_all(od, 'dcp', 1, 1, tiled=True)  4.73 us
    reduce_sum x1, other arithmetic, merge(): jnp.sum(wt[..., None] * od.astype(jnp.float32), axis=axis)  3.64 us
    all_to_all x1, starting transfers between devices, local(): lse = lax.all_to_all(lse, 'dcp', 1, 1, tiled=True)  3.54 us
  transfers between devices with their start and end apart: 3, of which 2 were waited for; matrix products, arithmetic and copies ran while one was open for 14% of the time, Pallas kernels for 0%

commit v1 on v0

v1 whole, which is shorter than its diff:
```python
import functools

import jax
import jax.numpy as jnp
from jax import lax
from jax.experimental import pallas as pl
from jax.experimental.pallas import tpu as pltpu
from jax.sharding import PartitionSpec as P

ROPE = 64
SCALE = 192 ** -0.5
F32 = jnp.float32
BF16 = jnp.bfloat16
NT = (((1,), (1,)), ((), ()))

SC = 4
H = SC // 2
QD = 3
D1, D2, D3 = 2, 3, 5

OWN, MATE, LEFT, RIGHT, OPP = 0, 1, 2, 4, 6

KINDS = ('QR', 'QL', 'FR', 'FL', 'ML', 'MR', 'MO', 'S1', 'S2', 'S3', 'S4', 'S5', 'S6', 'S7',
         'MA', 'MB', 'MC', 'HR0', 'HR1', 'HL0', 'HL1', 'DR0', 'DR1', 'DL0', 'DL1', 'AR', 'AL')
SEM = {k: i for i, k in enumerate(KINDS)}
LSE_TO = {'S1': (0, 1, MATE), 'S2': (1, 0, LEFT), 'S3': (1, 1, LEFT + 1), 'S4': (-1, 0, RIGHT),
          'S5': (-1, 1, RIGHT + 1), 'S6': (2, 0, OPP), 'S7': (2, 1, OPP + 1)}


def kernel(n, len_ref, q_hbm, c_hbm, o_hbm,
           q_v, c_v, o_v, lse_v, wrow, wt, m_a, m_b, m_c, h_p, h_n, d_p, d_n, a_p, a_n, r_p, r_n, out_v,
           send, recv, qm_sem, q_sem, c_sem, o_sem):
    G = q_v.shape[0]
    lat = o_v.shape[3]
    heads = o_v.shape[2]
    hl = heads // n
    sl = c_v.shape[2]
    nc = n // 2
    me = lax.axis_index('dcp')
    chip = lax.div(me, 2)
    core = lax.rem(me, 2)

    def dev(dx, other):
        return 2 * lax.rem(chip + dx + nc, nc) + (1 - core if other else core)

    def hd(d):
        return pl.ds(pl.multiple_of(d * hl, hl), hl)

    first, second, both = pl.ds(0, H), pl.ds(H, H), pl.ds(0, SC)
    right, left, opp, mate = dev(1, 0), dev(-1, 0), dev(2, 0), dev(0, 1)
    right1, left1, opp1 = dev(1, 1), dev(-1, 1), dev(2, 1)

    def same_q(g, part, d):
        r = q_v.at[g, part, hd(d)]
        return r, r

    def msg(kind, g):
        if kind == 'QR':
            src, dst = same_q(g, both, me)
            to = right
        elif kind == 'QL':
            src, dst = same_q(g, both, me)
            to = left
        elif kind == 'FR':
            src, dst = same_q(g, first, left)
            to = right
        elif kind == 'FL':
            src, dst = same_q(g, second, right)
            to = left
        elif kind == 'ML':
            src, dst = same_q(g, both, left)
            to = mate
        elif kind == 'MR':
            src, dst = same_q(g, both, right)
            to = mate
        elif kind == 'MO':
            src, dst = same_q(g, both, opp)
            to = mate
        elif kind in LSE_TO:
            dx, other, slot = LSE_TO[kind]
            src, dst, to = lse_v.at[OWN, g], lse_v.at[slot, g], dev(dx, other)
        elif kind == 'MA':
            src, dst, to = o_v.at[g, both, hd(mate)], m_a.at[g], mate
        elif kind == 'MB':
            src, dst, to = o_v.at[g, first, hd(right1)], m_b.at[g], mate
        elif kind == 'MC':
            src, dst, to = o_v.at[g, second, hd(left1)], m_c.at[g], mate
        elif kind == 'HR0':
            src, dst, to = o_v.at[g, first, hd(opp)], h_p.at[0, g], right
        elif kind == 'HR1':
            src, dst, to = o_v.at[g, first, hd(opp1)], h_p.at[1, g], right1
        elif kind == 'HL0':
            src, dst, to = o_v.at[g, second, hd(opp)], h_n.at[0, g], left
        elif kind == 'HL1':
            src, dst, to = o_v.at[g, second, hd(opp1)], h_n.at[1, g], left1
        elif kind == 'DR0':
            src, dst, to = o_v.at[g, second, hd(right)], d_p.at[0, g], right
        elif kind == 'DR1':
            src, dst, to = o_v.at[g, second, hd(right1)], d_p.at[1, g], right1
        elif kind == 'DL0':
            src, dst, to = o_v.at[g, first, hd(left)], d_n.at[0, g], left
        elif kind == 'DL1':
            src, dst, to = o_v.at[g, first, hd(left1)], d_n.at[1, g], left1
        elif kind == 'AR':
            src, dst, to = a_p.at[g], r_p.at[g], right
        else:
            src, dst, to = a_n.at[g], r_n.at[g], left
        i = SEM[kind]
        return pltpu.make_async_remote_copy(
            src_ref=src, dst_ref=dst, send_sem=send.at[i, g], recv_sem=recv.at[i, g],
            device_id={'dcp': to}, device_id_type=pl.DeviceIdType.MESH)

    def start(g, *kinds):
        for k in kinds:
            msg(k, g).start()

    def arrived(g, *kinds):
        for k in kinds:
            msg(k, g).wait_recv()

    def load(g, i):
        slot = lax.rem(g, 2) * SC + i
        return pltpu.make_async_copy(c_hbm.at[g, i], c_v.at[slot], c_sem.at[slot])

    def result(g):
        return pltpu.make_async_copy(out_v.at[g], o_hbm.at[g], o_sem.at[g])

    own = pltpu.make_async_copy(q_hbm, q_v.at[:, :, hd(me)], q_sem)
    own.start()
    for g in range(min(2, G)):
        for i in range(SC):
            load(g, i).start()
    wrow[...] = jnp.zeros_like(wrow)

    barrier = pltpu.get_barrier_semaphore()
    for d in (mate, right, right1, left, left1, opp, opp1):
        pl.semaphore_signal(barrier, inc=1, device_id={'dcp': d}, device_id_type=pl.DeviceIdType.MESH)
    pl.semaphore_wait(barrier, n - 1)
    own.wait()

    qm_ref = q_v.at[:, :, hd(me)]
    to_mate = pltpu.make_async_remote_copy(
        src_ref=qm_ref, dst_ref=qm_ref, send_sem=qm_sem.at[0], recv_sem=qm_sem.at[1],
        device_id={'dcp': mate}, device_id_type=pl.DeviceIdType.MESH)
    for g in range(min(QD, G)):
        start(g, 'QR', 'QL')
    to_mate.start()

    def attention(g):
        for i in range(SC):
            load(g, i).wait()
        pos = me * sl + lax.broadcasted_iota(jnp.int32, (1, sl), 1)
        lane = lax.broadcasted_iota(jnp.int32, (heads, 128), 1)
        lses = jnp.zeros((heads, 128), F32)
        for i in range(SC):
            c = c_v.at[lax.rem(g, 2) * SC + i]
            s = jnp.dot(q_v[g, i], c[...], preferred_element_type=F32)
            s = jnp.where(pos < len_ref[g * SC + i], s * SCALE, -jnp.inf)
            m = jnp.max(s, axis=1, keepdims=True)
            m0 = jnp.where(m > -jnp.inf, m, 0.0)
            p = jnp.exp(s - m0)
            l = jnp.sum(p, axis=1, keepdims=True)
            pv = lax.dot_general(p.astype(BF16), c[:lat], NT, preferred_element_type=F32)
            has = l > 0.0
            l1 = jnp.where(has, l, 1.0)
            o_v[g, i] = (pv * (1.0 / l1)).astype(BF16)
            lse = jnp.where(has, m0 + jnp.log(l1), -jnp.inf)
            lses = jnp.where(lane == i, lse, lses)
        lse_v[OWN, g] = lses.T[:SC]

    def weights(g):
        ls = [lse_v[s, g] for s in range(n)]
        mx = functools.reduce(jnp.maximum, ls)
        es = [jnp.exp(x - mx) for x in ls]
        z = 1.0 / functools.reduce(jnp.add, es)
        for s in range(n):
            wrow[s * SC:(s + 1) * SC, :] = es[s] * z
        wt[g] = wrow[...].T

    def weighted(w, slot, i, o):
        c = slot * SC + i
        return w[:, c:c + 1] * o.astype(F32)

    def partial_sums(g):
        w = wt[g, hd(right)]
        for i in range(H):
            a_p[g, i] = (weighted(w, OWN, i, o_v[g, i, hd(right)]) + weighted(w, MATE, i, m_b[g, i])
                         + weighted(w, LEFT, i, h_p[0, g, i]) + weighted(w, LEFT + 1, i, h_p[1, g, i]))
        w = wt[g, hd(left)]
        for i in range(H):
            a_n[g, i] = (weighted(w, OWN, H + i, o_v[g, H + i, hd(left)]) + weighted(w, MATE, H + i, m_c[g, i])
                         + weighted(w, RIGHT, H + i, h_n[0, g, i]) + weighted(w, RIGHT + 1, H + i, h_n[1, g, i]))

    def final(g):
        w = wt[g, hd(me)]
        for i in range(SC):
            o = weighted(w, OWN, i, o_v[g, i, hd(me)]) + weighted(w, MATE, i, m_a[g, i])
            if i < H:
                o += (r_p[g, i] + weighted(w, RIGHT, i, d_n[0, g, i]) + weighted(w, RIGHT + 1, i, d_n[1, g, i]))
            else:
                j = i - H
                o += (r_n[g, j] + weighted(w, LEFT, i, d_p[0, g, j]) + weighted(w, LEFT + 1, i, d_p[1, g, j]))
            out_v[g, i] = o.astype(BF16)

    def stage(t, lag, extra=0):
        g = t - lag
        return g, (g >= 0) & (g < G - extra)

    def step(t, carry):
        a, on = stage(t, 0)

        @pl.when(on)
        def _():
            arrived(a, 'QR', 'QL')
            start(a, 'FR', 'FL', 'ML', 'MR')

        @pl.when(stage(t, 0, QD)[1])
        def _():
            start(t + QD, 'QR', 'QL')

        b, on = stage(t, 1)

        @pl.when(on)
        def _():
            arrived(b, 'FR', 'FL')
            start(b, 'MO')

        @pl.when(t == 2)
        def _():
            to_mate.wait_recv()

        g, on = stage(t, 2)

        @pl.when(on)
        def _():
            arrived(g, 'ML', 'MR', 'MO')
            attention(g)
            start(g, 'HR0', 'HR1', 'HL0', 'HL1', 'MA', 'MB', 'MC', *LSE_TO)

        @pl.when(stage(t, 2, 2)[1])
        def _():
            for i in range(SC):
                load(t, i).start()

        d, on = stage(t, 2 + D1)

        @pl.when(on)
        def _():
            arrived(d, 'HR0', 'HR1', 'HL0', 'HL1', 'MB', 'MC', *LSE_TO)
            weights(d)
            partial_sums(d)
            start(d, 'AR', 'AL')

        e, on = stage(t, 2 + D2)

        @pl.when(on)
        def _():
            start(e, 'DR0', 'DR1', 'DL0', 'DL1')

        f, on = stage(t, 2 + D3)

        @pl.when(on)
        def _():
            arrived(f, 'MA', 'AR', 'AL', 'DR0', 'DR1', 'DL0', 'DL1')
            final(f)
            result(f).start()

        f, on = stage(t, 3 + D3)

        @pl.when(on)
        def _():
            for k in KINDS:
                msg(k, f).wait_send()
            result(f).wait()

        return carry

    lax.fori_loop(0, G + 4 + D3, step, 0)
    to_mate.wait_send()


def solution(mesh):
    n = mesh.shape['dcp']

    def local(q, cache, lengths):
        b, sl, wd = cache.shape
        hl = q.shape[1]
        heads = hl * n
        lat = wd - ROPE
        G = b // SC
        ct = jnp.swapaxes(cache, 1, 2).reshape(G, SC, wd, sl)
        vmem = pltpu.VMEM
        out = pl.pallas_call(
            functools.partial(kernel, n),
            out_shape=jax.ShapeDtypeStruct((G, SC, hl, lat), BF16),
            in_specs=[pl.BlockSpec(memory_space=pltpu.SMEM), pl.BlockSpec(memory_space=pl.ANY),
                      pl.BlockSpec(memory_space=pl.ANY)],
            out_specs=pl.BlockSpec(memory_space=pl.ANY),
            scratch_shapes=[
                vmem((G, SC, heads, wd), BF16),
                vmem((2 * SC, wd, sl), BF16),
                vmem((G, SC, heads, lat), BF16),
                vmem((n, G, SC, heads), F32),
                vmem((128, heads), F32),
                vmem((G, heads, 128), F32),
                vmem((G, SC, hl, lat), BF16),
                vmem((G, H, hl, lat), BF16),
                vmem((G, H, hl, lat), BF16),
                vmem((2, G, H, hl, lat), BF16),
                vmem((2, G, H, hl, lat), BF16),
                vmem((2, G, H, hl, lat), BF16),
                vmem((2, G, H, hl, lat), BF16),
                vmem((G, H, hl, lat), F32),
                vmem((G, H, hl, lat), F32),
                vmem((G, H, hl, lat), F32),
                vmem((G, H, hl, lat), F32),
                vmem((G, SC, hl, lat), BF16),
                pltpu.SemaphoreType.DMA((len(KINDS), G)),
                pltpu.SemaphoreType.DMA((len(KINDS), G)),
                pltpu.SemaphoreType.DMA((2,)),
                pltpu.SemaphoreType.DMA,
                pltpu.SemaphoreType.DMA((2 * SC,)),
                pltpu.SemaphoreType.DMA((G,)),
            ],
            compiler_params=pltpu.CompilerParams(
                collective_id=0, has_side_effects=True, vmem_limit_bytes=56 * 2 ** 20),
        )(lengths, q.reshape(G, SC, hl, wd), ct)
        return out.reshape(b, hl, lat)

    return jax.shard_map(local, mesh=mesh, in_specs=(P('dp', 'dcp', None), P('dp', 'dcp', None), P('dp')),
                         out_specs=P('dp', 'dcp', None), check_vma=False)
```

time: 165 us -> 73.7 us (0.45)
  waiting for transfers between devices: 85.5 us -> 0 us
  Pallas kernels: 0 us -> 70.6 us
  matrix products: 39.5 us -> 0 us
  between operations: 13.5 us -> 0.01 us
  other arithmetic: 13.2 us -> 0 us
  starting transfers between devices: 8.27 us -> 0 us
  local copies, waits for them, and re-layouts: 4.01 us -> 1.87 us
    pallas_call x0 -> x1, Pallas kernels: none -> 70.6 us  [local(): pl.pallas_call(functools.partial(kernel, n), out_shape=jax.ShapeDtypeStru...]
    all_to_all x2 -> x0, waiting for transfers between devices: 48 us -> none  [the longest x1 48 us: local(): od = lax.all_to_all(od, 'dcp', 1, 1, tiled=True)]
    dot_general x2 -> x0, matrix products: 39.5 us -> none  [the longest x1 20.5 us: partial_attention(): jnp.einsum('bhk,btk->bht', q, blk, preferred_element_type=jnp.float32)]
    all_gather x1 -> x0, waiting for transfers between devices: 36.7 us -> none  [local(): qa = lax.all_gather(q, 'dcp', axis=1, tiled=True)]
    reduce_sum x3 -> x0, other arithmetic: 11.7 us -> none  [the longest x1 8.03 us: partial_attention(): l = jnp.sum(p, axis=2)]
    all_to_all x2 -> x0, starting transfers between devices: 8.27 us -> none  [the longest x1 4.73 us: local(): od = lax.all_to_all(od, 'dcp', 1, 1, tiled=True)]
    reshape x1 -> x0, local copies, waits for them, and re-layouts: 2.44 us -> none  [local(): od = od.reshape(b, n, h // n, lat)]
  transfers between devices with their start and end apart: 3 -> 0, of which waited for: 2 -> 0; matrix products, arithmetic and copies ran while one was open for 14% -> 0% of each run, Pallas kernels for 0% -> 0%
where the time goes in v1:
time: 73.7 us; the launch traced here: 72.5 us
  Pallas kernels  70.6 us (96%)
  local copies, waits for them, and re-layouts  1.87 us (3%)
    pallas_call x1, Pallas kernels, local(): pl.pallas_call(functools.partial(kernel, n), out_shape=jax.ShapeDtypeStru...  70.6 us
    unnamed x1, local copies, waits for them, and re-layouts  1.87 us

profile of v1, /device:TPU:88, one launch (start us, length us, event | category | flops | bytes accessed | tf_op | source)
XLA Modules:
  0.0 72.5 jit_solution(11916211253014239722)
XLA Ops:
  0.0 70.6 %shard_map.37 = bf16[8,4,16,512]{3,2,1,0:T(8,128)(2,1)} custom-call(s32[32]{0:T(128)} %len_ref.1, bf16[8,4,16,576]{3,2,1,0:T(8,128)(2,1)} %bitcast.7, bf16[8,4,576,1024]{3,2,1,0:T(8,128)(2,1)} %bitcast.5), custom_call_target="tpu_custom_call" | custom-call | tf_op jit(solution)/shard_map/pallas_call | solution.py:293
  70.6 1.9 %copy.5 = bf16[32,16,512]{2,1,0:T(8,128)(2,1)} copy(bf16[32,16,512]{2,1,0:T(8,128)(2,1)} %bitcast.6) | data formatting | bytes 1048576

commit v2 on v1

v2 whole, which is shorter than its diff:
```python
import functools

import jax
import jax.numpy as jnp
from jax import lax
from jax.experimental import pallas as pl
from jax.experimental.pallas import tpu as pltpu
from jax.sharding import PartitionSpec as P

ROPE = 64
SCALE = 192 ** -0.5
F32 = jnp.float32
BF16 = jnp.bfloat16
NT = (((1,), (1,)), ((), ()))

SC = 4
H = SC // 2
QD = 3
D1, D2 = 2, 2

OWN, MATE, LEFT, RIGHT = 0, 1, 2, 4

KINDS = ('QR', 'QL', 'FR', 'FL', 'ML', 'MR', 'MO', 'QM', 'S1', 'S2', 'S3', 'S4', 'S5', 'TR', 'TL',
         'MA', 'MB', 'MC', 'HR0', 'HR1', 'HL0', 'HL1', 'DR0', 'DR1', 'DL0', 'DL1', 'AR', 'AL')
SEM = {k: i for i, k in enumerate(KINDS)}
LSE_TO = {'S1': (0, 1, MATE), 'S2': (1, 0, LEFT), 'S3': (1, 1, LEFT + 1), 'S4': (-1, 0, RIGHT),
          'S5': (-1, 1, RIGHT + 1)}


def kernel(n, len_hbm, q_hbm, c_hbm, out_v,
           len_ref, q_st, q_v, c_v, o_v, lse_v, t_s, t_r, wrow, wt, m_a, m_b, m_c, h_p, h_n, d_p, d_n, a_p, a_n, r_p, r_n,
           send, recv, len_sem, q_sem, c_sem):
    G = q_v.shape[0]
    lat = o_v.shape[3]
    heads = o_v.shape[2]
    hl = heads // n
    sl = c_v.shape[2]
    nc = n // 2
    me = lax.axis_index('dcp')
    chip = lax.div(me, 2)
    core = lax.rem(me, 2)

    def dev(dx, other):
        return 2 * lax.rem(chip + dx + nc, nc) + (1 - core if other else core)

    def hd(d):
        return pl.ds(pl.multiple_of(d * hl, hl), hl)

    first, second, both = pl.ds(0, H), pl.ds(H, H), pl.ds(0, SC)
    pairs, pairs1, pairs2 = pl.ds(0, H), pl.ds(0, H // 2), pl.ds(H // 2, H // 2)
    right, left, opp, mate = dev(1, 0), dev(-1, 0), dev(2, 0), dev(0, 1)
    right1, left1, opp1 = dev(1, 1), dev(-1, 1), dev(2, 1)

    def same_q(g, part, d):
        r = q_v.at[g, part, hd(d)]
        return r, r

    def msg(kind, g):
        if kind == 'QR':
            src, dst = same_q(g, pairs, me)
            to = right
        elif kind == 'QL':
            src, dst = same_q(g, pairs, me)
            to = left
        elif kind == 'FR':
            src, dst = same_q(g, pairs1, left)
            to = right
        elif kind == 'FL':
            src, dst = same_q(g, pairs2, right)
            to = left
        elif kind == 'ML':
            src, dst = same_q(g, pairs, left)
            to = mate
        elif kind == 'MR':
            src, dst = same_q(g, pairs, right)
            to = mate
        elif kind == 'MO':
            src, dst = same_q(g, pairs, opp)
            to = mate
        elif kind == 'QM':
            src, dst = same_q(g, pairs, me)
            to = mate
        elif kind == 'TR':
            src, dst, to = t_s.at[0, g], t_r.at[0, g], right
        elif kind == 'TL':
            src, dst, to = t_s.at[1, g], t_r.at[1, g], left
        elif kind in LSE_TO:
            dx, other, slot = LSE_TO[kind]
            src, dst, to = lse_v.at[OWN, g], lse_v.at[slot, g], dev(dx, other)
        elif kind == 'MA':
            src, dst, to = o_v.at[g, both, hd(mate)], m_a.at[g], mate
        elif kind == 'MB':
            src, dst, to = o_v.at[g, first, hd(right1)], m_b.at[g], mate
        elif kind == 'MC':
            src, dst, to = o_v.at[g, second, hd(left1)], m_c.at[g], mate
        elif kind == 'HR0':
            src, dst, to = o_v.at[g, first, hd(opp)], h_p.at[0, g], right
        elif kind == 'HR1':
            src, dst, to = o_v.at[g, first, hd(opp1)], h_p.at[1, g], right1
        elif kind == 'HL0':
            src, dst, to = o_v.at[g, second, hd(opp)], h_n.at[0, g], left
        elif kind == 'HL1':
            src, dst, to = o_v.at[g, second, hd(opp1)], h_n.at[1, g], left1
        elif kind == 'DR0':
            src, dst, to = o_v.at[g, second, hd(right)], d_p.at[0, g], right
        elif kind == 'DR1':
            src, dst, to = o_v.at[g, second, hd(right1)], d_p.at[1, g], right1
        elif kind == 'DL0':
            src, dst, to = o_v.at[g, first, hd(left)], d_n.at[0, g], left
        elif kind == 'DL1':
            src, dst, to = o_v.at[g, first, hd(left1)], d_n.at[1, g], left1
        elif kind == 'AR':
            src, dst, to = a_p.at[g], r_p.at[g], right
        else:
            src, dst, to = a_n.at[g], r_n.at[g], left
        i = SEM[kind]
        return pltpu.make_async_remote_copy(
            src_ref=src, dst_ref=dst, send_sem=send.at[i, g], recv_sem=recv.at[i, g],
            device_id={'dcp': to}, device_id_type=pl.DeviceIdType.MESH)

    def start(g, *kinds):
        for k in kinds:
            msg(k, g).start()

    def arrived(g, *kinds):
        for k in kinds:
            msg(k, g).wait_recv()

    def load(g, i):
        slot = lax.rem(g, 2) * SC + i
        return pltpu.make_async_copy(c_hbm.at[g, i], c_v.at[slot], c_sem.at[slot])

    barrier = pltpu.get_barrier_semaphore()
    for d in (mate, right, right1, left, left1):
        pl.semaphore_signal(barrier, inc=1, device_id={'dcp': d}, device_id_type=pl.DeviceIdType.MESH)

    def fetch(g):
        return pltpu.make_async_copy(q_hbm.at[g], q_st.at[g], q_sem.at[g])

    def fetch_start(g, carry):
        fetch(g).start()
        return carry

    lax.fori_loop(0, G, fetch_start, 0)
    lens = pltpu.make_async_copy(len_hbm, len_ref, len_sem)
    lens.start()
    for g in range(min(2, G)):
        for i in range(SC):
            load(g, i).start()
    wrow[...] = jnp.zeros_like(wrow)

    def pack(g):
        fetch(g).wait()
        for p in range(H):
            a, b = q_st[g, 2 * p], q_st[g, 2 * p + 1]
            q_v[g, p, hd(me), :lat] = a[:, :lat]
            q_v[g, p, hd(me), lat:2 * lat] = b[:, :lat]
            q_v[g, p, hd(me), 2 * lat:] = jnp.concatenate([a[:, lat:], b[:, lat:]], axis=1)

    for g in range(min(QD, G)):
        pack(g)
    lens.wait()
    pl.semaphore_wait(barrier, 5)
    for g in range(min(QD, G)):
        start(g, 'QR', 'QL', 'QM')

    def attention(g):
        for i in range(SC):
            load(g, i).wait()
        pos = me * sl + lax.broadcasted_iota(jnp.int32, (1, sl), 1)
        lane = lax.broadcasted_iota(jnp.int32, (heads, 128), 1)
        lses = jnp.zeros((heads, 128), F32)
        for i in range(SC):
            c = c_v.at[lax.rem(g, 2) * SC + i]
            p, r = divmod(i, 2)
            rope = q_v[g, p, :, 2 * lat + r * ROPE:2 * lat + (r + 1) * ROPE]
            s = (jnp.dot(q_v[g, p, :, r * lat:(r + 1) * lat], c[:lat], preferred_element_type=F32)
                 + jnp.dot(rope, c[lat:], preferred_element_type=F32))
            s = jnp.where(pos < len_ref[g * SC + i], s * SCALE, -jnp.inf)
            m = jnp.max(s, axis=1, keepdims=True)
            m0 = jnp.where(m > -jnp.inf, m, 0.0)
            p = jnp.exp(s - m0)
            l = jnp.sum(p, axis=1, keepdims=True)
            pv = lax.dot_general(p.astype(BF16), c[:lat], NT, preferred_element_type=F32)
            has = l > 0.0
            l1 = jnp.where(has, l, 1.0)
            o_v[g, i] = (pv * (1.0 / l1)).astype(BF16)
            lse = jnp.where(has, m0 + jnp.log(l1), -jnp.inf)
            lses = jnp.where(lane == i, lse, lses)
        lse_v[OWN, g] = lses.T[:SC]

    row = lax.broadcasted_iota(jnp.int32, (SC, heads), 0)

    def softmax(ls):
        mx = functools.reduce(jnp.maximum, ls)
        mx = jnp.where(mx > -jnp.inf, mx, 0.0)
        es = [jnp.exp(x - mx) for x in ls]
        z = functools.reduce(jnp.add, es)
        has = z > 0.0
        z1 = jnp.where(has, z, 1.0)
        r = 1.0 / z1
        for k, e in enumerate(es):
            wrow[k * SC:(k + 1) * SC, :] = e * r
        wt[...] = wrow[...].T
        return jnp.where(has, mx + jnp.log(z1), -jnp.inf)

    def near(g, k, a, b):
        return jnp.where(row < H, lse_v[a + k, g], lse_v[b + k, g])

    def weighted(w, k, i, o):
        c = k * SC + i
        return w[:, c:c + 1] * o.astype(F32)

    def partial_sums(g):
        t = softmax([lse_v[OWN, g], lse_v[MATE, g], near(g, 0, LEFT, RIGHT), near(g, 1, LEFT, RIGHT)])
        t_s[0, g] = t[:H]
        t_s[1, g] = t[H:]
        for first_half, d, m, h, a in ((True, right, m_b, h_p, a_p), (False, left, m_c, h_n, a_n)):
            w = wt[hd(d)]
            for j in range(H):
                i = j if first_half else H + j
                a[g, j] = (weighted(w, 0, i, o_v[g, i, hd(d)]) + weighted(w, 1, i, m[g, j])
                           + weighted(w, 2, i, h[0, g, j]) + weighted(w, 3, i, h[1, g, j]))

    def final(g):
        far = jnp.concatenate([t_r[0, g], t_r[1, g]], axis=0)
        softmax([lse_v[OWN, g], lse_v[MATE, g], near(g, 0, RIGHT, LEFT), near(g, 1, RIGHT, LEFT), far])
        w = wt[hd(me)]
        for i in range(SC):
            d, r, j = (d_n, r_p, i) if i < H else (d_p, r_n, i - H)
            out_v[g, i] = (weighted(w, 0, i, o_v[g, i, hd(me)]) + weighted(w, 1, i, m_a[g, i])
                           + weighted(w, 2, i, d[0, g, j]) + weighted(w, 3, i, d[1, g, j])
                           + weighted(w, 4, i, r[g, j])).astype(BF16)

    def stage(t, lag, extra=0):
        g = t - lag
        return g, (g >= 0) & (g < G - extra)

    def step(t, carry):
        a, on = stage(t, 0)

        @pl.when(on)
        def _():
            arrived(a, 'QR', 'QL')
            start(a, 'FR', 'FL', 'ML', 'MR')

        @pl.when(stage(t, 0, QD)[1])
        def _():
            pack(t + QD)
            start(t + QD, 'QR', 'QL', 'QM')

        b, on = stage(t, 1)

        @pl.when(on)
        def _():
            arrived(b, 'FR', 'FL')
            start(b, 'MO')

        g, on = stage(t, 2)

        @pl.when(on)
        def _():
            arrived(g, 'QM', 'ML', 'MR', 'MO')
            attention(g)
            start(g, 'HR0', 'HR1', 'HL0', 'HL1', 'MA', 'MB', 'MC', *LSE_TO)

        @pl.when(stage(t, 2, 2)[1])
        def _():
            for i in range(SC):
                load(t, i).start()

        d, on = stage(t, 2 + D1)

        @pl.when(on)
        def _():
            sums(d)

        e, on = stage(t, 2 + D2)

        @pl.when(on)
        def _():
            start(e, 'DR0', 'DR1', 'DL0', 'DL1')

        return carry

    def sums(g):
        arrived(g, 'HR0', 'HR1', 'HL0', 'HL1', 'MB', 'MC', *LSE_TO)
        partial_sums(g)
        start(g, 'AR', 'AL', 'TR', 'TL')

    lax.fori_loop(0, G + 2, step, 0)

    def direct(g, carry):
        start(g, 'DR0', 'DR1', 'DL0', 'DL1')
        return carry

    lax.fori_loop(G - D2, G, direct, 0)

    def rest(g, carry):
        sums(g)
        return carry

    lax.fori_loop(G - D1, G, rest, 0)

    def sent(g):
        for k in KINDS:
            msg(k, g).wait_send()

    def finish(g, carry):
        @pl.when(g >= 1)
        def _():
            sent(g - 1)

        arrived(g, 'MA', 'AR', 'AL', 'TR', 'TL', 'DR0', 'DR1', 'DL0', 'DL1')
        final(g)
        return carry

    lax.fori_loop(0, G, finish, 0)
    sent(G - 1)


def solution(mesh):
    n = mesh.shape['dcp']

    def local(q, cache, lengths):
        b, sl, wd = cache.shape
        hl = q.shape[1]
        heads = hl * n
        lat = wd - ROPE
        G = b // SC
        ct = jnp.swapaxes(cache, 1, 2).reshape(G, SC, wd, sl)
        vmem = pltpu.VMEM
        out = pl.pallas_call(
            functools.partial(kernel, n),
            out_shape=vmem((G, SC, hl, lat), BF16),
            in_specs=[pl.BlockSpec(memory_space=pl.ANY)] * 3,
            out_specs=pl.BlockSpec(memory_space=pltpu.VMEM),
            scratch_shapes=[
                pltpu.SMEM((b,), jnp.int32),
                vmem((G, SC, hl, wd), BF16),
                vmem((G, H, heads, 2 * wd), BF16),
                vmem((2 * SC, wd, sl), BF16),
                vmem((G, SC, heads, lat), BF16),
                vmem((6, G, SC, heads), F32),
                vmem((2, G, H, heads), F32),
                vmem((2, G, H, heads), F32),
                vmem((128, heads), F32),
                vmem((heads, 128), F32),
                vmem((G, SC, hl, lat), BF16),
                vmem((G, H, hl, lat), BF16),
                vmem((G, H, hl, lat), BF16),
                vmem((2, G, H, hl, lat), BF16),
                vmem((2, G, H, hl, lat), BF16),
                vmem((2, G, H, hl, lat), BF16),
                vmem((2, G, H, hl, lat), BF16),
                vmem((G, H, hl, lat), F32),
                vmem((G, H, hl, lat), F32),
                vmem((G, H, hl, lat), F32),
                vmem((G, H, hl, lat), F32),
                pltpu.SemaphoreType.DMA((len(KINDS), G)),
                pltpu.SemaphoreType.DMA((len(KINDS), G)),
                pltpu.SemaphoreType.DMA,
                pltpu.SemaphoreType.DMA((G,)),
                pltpu.SemaphoreType.DMA((2 * SC,)),
            ],
            compiler_params=pltpu.CompilerParams(
                collective_id=0, has_side_effects=True, vmem_limit_bytes=56 * 2 ** 20),
        )(lengths, q.reshape(G, SC, hl, wd), ct)
        return out.reshape(b, hl, lat)

    return jax.shard_map(local, mesh=mesh, in_specs=(P('dp', 'dcp', None), P('dp', 'dcp', None), P('dp')),
                         out_specs=P('dp', 'dcp', None), check_vma=False)
```

time: 73.7 us -> 66.2 us (0.90); the launches traced: 72.5 us -> 66.1 us
  Pallas kernels: 70.6 us -> 65.3 us
  local copies, waits for them, and re-layouts: 1.87 us -> 0.8 us
    pallas_call x1, Pallas kernels: 70.6 us -> 65.3 us  [local(): pl.pallas_call(functools.partial(kernel, n), out_shape=vmem((G, SC, hl, l...]
    unnamed x1, local copies, waits for them, and re-layouts: 1.87 us -> 0.8 us
where the time goes in v2:
time: 66.2 us; the launch traced here: 66.1 us
  Pallas kernels  65.3 us (99%)
  local copies, waits for them, and re-layouts  0.8 us (1%)
    pallas_call x1, Pallas kernels, local(): pl.pallas_call(functools.partial(kernel, n), out_shape=vmem((G, SC, hl, l...  65.3 us

profile of v2, /device:TPU:88, one launch (start us, length us, event | category | flops | bytes accessed | tf_op | source)
XLA Modules:
  0.0 66.1 jit_solution(5727797432391818170)
XLA Ops:
  0.0 65.3 %shard_map.37 = bf16[8,4,16,512]{3,2,1,0:T(8,128)(2,1)S(1)} custom-call(s32[32]{0:T(128)} %len_hbm.1, bf16[8,4,16,576]{3,2,1,0:T(8,128)(2,1)} %bitcast.7, bf16[8,4,576,1024]{3,2,1,0:T(8,128)(2,1)} %bitcast.6), custom_call_target="tpu_custom_call" | custom-call | tf_op jit(solution)/shard_map/pallas_call | solution.py:333
  65.3 0.8 %copy.5 = bf16[32,16,512]{2,1,0:T(8,128)(2,1)} copy(bf16[32,16,512]{2,1,0:T(8,128)(2,1)S(1)} %bitcast.5) | data formatting | bytes 1048576

commit v3 on v2

--- a/solution.py
+++ b/solution.py
@@ -15,6 +15,7 @@
 
 SC = 4
 H = SC // 2
+OWN_AT = {6: 2}
 QD = 3
 D1, D2 = 2, 2
 
@@ -170,12 +171,18 @@
         pos = me * sl + lax.broadcasted_iota(jnp.int32, (1, sl), 1)
         lane = lax.broadcasted_iota(jnp.int32, (heads, 128), 1)
         lses = jnp.zeros((heads, 128), F32)
-        for i in range(SC):
+
+        def scores(i):
             c = c_v.at[lax.rem(g, 2) * SC + i]
             p, r = divmod(i, 2)
             rope = q_v[g, p, :, 2 * lat + r * ROPE:2 * lat + (r + 1) * ROPE]
-            s = (jnp.dot(q_v[g, p, :, r * lat:(r + 1) * lat], c[:lat], preferred_element_type=F32)
-                 + jnp.dot(rope, c[lat:], preferred_element_type=F32))
+            return (jnp.dot(q_v[g, p, :, r * lat:(r + 1) * lat], c[:lat], preferred_element_type=F32)
+                    + jnp.dot(rope, c[lat:], preferred_element_type=F32))
+
+        ahead = scores(0)
+        for i in range(SC):
+            c = c_v.at[lax.rem(g, 2) * SC + i]
+            s, ahead = ahead, scores(i + 1) if i + 1 < SC else None
             s = jnp.where(pos < len_ref[g * SC + i], s * SCALE, -jnp.inf)
             m = jnp.max(s, axis=1, keepdims=True)
             m0 = jnp.where(m > -jnp.inf, m, 0.0)
@@ -244,10 +251,11 @@
             arrived(a, 'QR', 'QL')
             start(a, 'FR', 'FL', 'ML', 'MR')
 
-        @pl.when(stage(t, 0, QD)[1])
-        def _():
-            pack(t + QD)
-            start(t + QD, 'QR', 'QL', 'QM')
+        for h in range(QD, G):
+            @pl.when(t == OWN_AT.get(h, h - QD))
+            def _():
+                pack(h)
+                start(h, 'QR', 'QL', 'QM')
 
         b, on = stage(t, 1)
 
@@ -255,6 +263,12 @@
         def _():
             arrived(b, 'FR', 'FL')
             start(b, 'MO')
+
+        e, on = stage(t, 2 + D2)
+
+        @pl.when(on)
+        def _():
+            start(e, 'DR0', 'DR1', 'DL0', 'DL1')
 
         g, on = stage(t, 2)
 
@@ -274,12 +288,6 @@
         @pl.when(on)
         def _():
             sums(d)
-
-        e, on = stage(t, 2 + D2)
-
-        @pl.when(on)
-        def _():
-            start(e, 'DR0', 'DR1', 'DL0', 'DL1')
 
         return carry
 

time: 66.2 us -> 64.3 us (0.971)
  Pallas kernels: 65.3 us -> 63.4 us
    pallas_call x1, Pallas kernels: 65.3 us -> 63.4 us  [local(): pl.pallas_call(functools.partial(kernel, n), out_shape=vmem((G, SC, hl, l...]
where the time goes in v3:
time: 64.3 us; the launch traced here: 64.2 us
  Pallas kernels  63.4 us (99%)
  local copies, waits for them, and re-layouts  0.8 us (1%)
    pallas_call x1, Pallas kernels, local(): pl.pallas_call(functools.partial(kernel, n), out_shape=vmem((G, SC, hl, l...  63.4 us

profile of v3, /device:TPU:88, one launch (start us, length us, event | category | flops | bytes accessed | tf_op | source)
XLA Modules:
  0.0 64.2 jit_solution(9603226787617310185)
XLA Ops:
  0.0 63.4 %shard_map.37 = bf16[8,4,16,512]{3,2,1,0:T(8,128)(2,1)S(1)} custom-call(s32[32]{0:T(128)} %len_hbm.1, bf16[8,4,16,576]{3,2,1,0:T(8,128)(2,1)} %bitcast.7, bf16[8,4,576,1024]{3,2,1,0:T(8,128)(2,1)} %bitcast.6), custom_call_target="tpu_custom_call" | custom-call | tf_op jit(solution)/shard_map/pallas_call | solution.py:341
  63.4 0.8 %copy.5 = bf16[32,16,512]{2,1,0:T(8,128)(2,1)} copy(bf16[32,16,512]{2,1,0:T(8,128)(2,1)S(1)} %bitcast.5) | data formatting | bytes 1048576

commit v4 on v3

--- a/solution.py
+++ b/solution.py
@@ -15,21 +15,18 @@
 
 SC = 4
 H = SC // 2
-OWN_AT = {6: 2}
+OWN_AT = {6: 2, 7: 3}
 QD = 3
 D1, D2 = 2, 2
 
-OWN, MATE, LEFT, RIGHT = 0, 1, 2, 4
+ROWS = ((1, -1), (0, 0), (2, 1), (-1, 2))
 
 KINDS = ('QR', 'QL', 'FR', 'FL', 'ML', 'MR', 'MO', 'QM', 'S1', 'S2', 'S3', 'S4', 'S5', 'TR', 'TL',
          'MA', 'MB', 'MC', 'HR0', 'HR1', 'HL0', 'HL1', 'DR0', 'DR1', 'DL0', 'DL1', 'AR', 'AL')
 SEM = {k: i for i, k in enumerate(KINDS)}
-LSE_TO = {'S1': (0, 1, MATE), 'S2': (1, 0, LEFT), 'S3': (1, 1, LEFT + 1), 'S4': (-1, 0, RIGHT),
-          'S5': (-1, 1, RIGHT + 1)}
-
 
 def kernel(n, len_hbm, q_hbm, c_hbm, out_v,
-           len_ref, q_st, q_v, c_v, o_v, lse_v, t_s, t_r, wrow, wt, m_a, m_b, m_c, h_p, h_n, d_p, d_n, a_p, a_n, r_p, r_n,
+           len_ref, q_st, q_v, c_v, o_v, lse_c, z_own, z_mate, y_s, y_l, y_r, t_s, t_l, t_r, wrow, wt, m_a, m_b, m_c, h_p, h_n, d_p, d_n, a_p, a_n, r_p, r_n,
            send, recv, len_sem, q_sem, c_sem):
     G = q_v.shape[0]
     lat = o_v.shape[3]
@@ -82,12 +79,19 @@
             src, dst = same_q(g, pairs, me)
             to = mate
         elif kind == 'TR':
-            src, dst, to = t_s.at[0, g], t_r.at[0, g], right
+            src, dst, to = t_s.at[g], t_l.at[g], right
         elif kind == 'TL':
-            src, dst, to = t_s.at[1, g], t_r.at[1, g], left
-        elif kind in LSE_TO:
-            dx, other, slot = LSE_TO[kind]
-            src, dst, to = lse_v.at[OWN, g], lse_v.at[slot, g], dev(dx, other)
+            src, dst, to = t_s.at[g], t_r.at[g], left
+        elif kind == 'S1':
+            src, dst, to = z_own.at[g], z_mate.at[g], mate
+        elif kind == 'S2':
+            src, dst, to = y_s.at[0, g], y_l.at[0, g], right
+        elif kind == 'S3':
+            src, dst, to = y_s.at[0, g], y_l.at[1, g], right1
+        elif kind == 'S4':
+            src, dst, to = y_s.at[1, g], y_r.at[0, g], left
+        elif kind == 'S5':
+            src, dst, to = y_s.at[1, g], y_r.at[1, g], left1
         elif kind == 'MA':
             src, dst, to = o_v.at[g, both, hd(mate)], m_a.at[g], mate
         elif kind == 'MB':
@@ -160,17 +164,15 @@
 
     for g in range(min(QD, G)):
         pack(g)
+        if g == 0:
+            pl.semaphore_wait(barrier, 5)
+        start(g, 'QR', 'QL', 'QM')
     lens.wait()
-    pl.semaphore_wait(barrier, 5)
-    for g in range(min(QD, G)):
-        start(g, 'QR', 'QL', 'QM')
 
     def attention(g):
         for i in range(SC):
             load(g, i).wait()
         pos = me * sl + lax.broadcasted_iota(jnp.int32, (1, sl), 1)
-        lane = lax.broadcasted_iota(jnp.int32, (heads, 128), 1)
-        lses = jnp.zeros((heads, 128), F32)
 
         def scores(i):
             c = c_v.at[lax.rem(g, 2) * SC + i]
@@ -192,11 +194,21 @@
             has = l > 0.0
             l1 = jnp.where(has, l, 1.0)
             o_v[g, i] = (pv * (1.0 / l1)).astype(BF16)
-            lse = jnp.where(has, m0 + jnp.log(l1), -jnp.inf)
-            lses = jnp.where(lane == i, lse, lses)
-        lse_v[OWN, g] = lses.T[:SC]
-
-    row = lax.broadcasted_iota(jnp.int32, (SC, heads), 0)
+            lse_c[i] = jnp.broadcast_to(jnp.where(has, m0 + jnp.log(l1), -jnp.inf), (heads, 128))
+        lane = lax.broadcasted_iota(jnp.int32, (2 * hl, 128), 1)
+        columns = []
+        for i in range(SC):
+            block = jnp.zeros((2 * hl, 128), F32)
+            for r, steps in enumerate(ROWS):
+                c = lax.rem(chip + steps[i // H] + nc, nc)
+                block = jnp.where(lane == r, lse_c[i, pl.ds(pl.multiple_of(c * 2 * hl, 2 * hl), 2 * hl)], block)
+            columns.append(block)
+        rows = jnp.concatenate(columns, axis=0).T
+        z_own[g] = rows[:2]
+        y_s[0, g] = rows[2:3]
+        y_s[1, g] = rows[3:4]
+
+    early = lax.broadcasted_iota(jnp.int32, (1, 128), 1) < 2 * hl * H
 
     def softmax(ls):
         mx = functools.reduce(jnp.maximum, ls)
@@ -207,37 +219,36 @@
         z1 = jnp.where(has, z, 1.0)
         r = 1.0 / z1
         for k, e in enumerate(es):
-            wrow[k * SC:(k + 1) * SC, :] = e * r
+            wrow[k:k + 1, :] = e * r
         wt[...] = wrow[...].T
         return jnp.where(has, mx + jnp.log(z1), -jnp.inf)
 
-    def near(g, k, a, b):
-        return jnp.where(row < H, lse_v[a + k, g], lse_v[b + k, g])
-
-    def weighted(w, k, i, o):
-        c = k * SC + i
-        return w[:, c:c + 1] * o.astype(F32)
-
-    def partial_sums(g):
-        t = softmax([lse_v[OWN, g], lse_v[MATE, g], near(g, 0, LEFT, RIGHT), near(g, 1, LEFT, RIGHT)])
-        t_s[0, g] = t[:H]
-        t_s[1, g] = t[H:]
-        for first_half, d, m, h, a in ((True, right, m_b, h_p, a_p), (False, left, m_c, h_n, a_n)):
-            w = wt[hd(d)]
+    def weighted(k, i, o):
+        w = wt[pl.ds(pl.multiple_of((2 * i + core) * hl, hl), hl)]
+        return w[:, k:k + 1] * o.astype(F32)
+
+    def sums(g):
+        arrived(g, 'S1', 'S2', 'S3', 'S4', 'S5')
+        t_s[g] = softmax([z_own[g, 0:1], z_mate[g, 0:1]] + [jnp.where(early, y_l[k, g], y_r[k, g]) for k in range(2)])
+        start(g, 'TR', 'TL')
+        arrived(g, 'HR0', 'HR1', 'HL0', 'HL1', 'MB', 'MC')
+        for i0, d, m, h, a in ((0, right, m_b, h_p, a_p), (H, left, m_c, h_n, a_n)):
             for j in range(H):
-                i = j if first_half else H + j
-                a[g, j] = (weighted(w, 0, i, o_v[g, i, hd(d)]) + weighted(w, 1, i, m[g, j])
-                           + weighted(w, 2, i, h[0, g, j]) + weighted(w, 3, i, h[1, g, j]))
+                i = i0 + j
+                a[g, j] = (weighted(0, i, o_v[g, i, hd(d)]) + weighted(1, i, m[g, j])
+                           + weighted(2, i, h[0, g, j]) + weighted(3, i, h[1, g, j]))
+        start(g, 'AR', 'AL')
 
     def final(g):
-        far = jnp.concatenate([t_r[0, g], t_r[1, g]], axis=0)
-        softmax([lse_v[OWN, g], lse_v[MATE, g], near(g, 0, RIGHT, LEFT), near(g, 1, RIGHT, LEFT), far])
-        w = wt[hd(me)]
+        arrived(g, 'MA', 'TR', 'TL')
+        softmax([z_own[g, 1:2], z_mate[g, 1:2]] + [jnp.where(early, y_r[k, g], y_l[k, g]) for k in range(2)]
+                + [jnp.where(early, t_l[g], t_r[g])])
+        arrived(g, 'DR0', 'DR1', 'DL0', 'DL1', 'AR', 'AL')
         for i in range(SC):
             d, r, j = (d_n, r_p, i) if i < H else (d_p, r_n, i - H)
-            out_v[g, i] = (weighted(w, 0, i, o_v[g, i, hd(me)]) + weighted(w, 1, i, m_a[g, i])
-                           + weighted(w, 2, i, d[0, g, j]) + weighted(w, 3, i, d[1, g, j])
-                           + weighted(w, 4, i, r[g, j])).astype(BF16)
+            out_v[g, i] = (weighted(0, i, o_v[g, i, hd(me)]) + weighted(1, i, m_a[g, i])
+                           + weighted(2, i, d[0, g, j]) + weighted(3, i, d[1, g, j])
+                           + weighted(4, i, r[g, j])).astype(BF16)
 
     def stage(t, lag, extra=0):
         g = t - lag
@@ -276,7 +287,7 @@
         def _():
             arrived(g, 'QM', 'ML', 'MR', 'MO')
             attention(g)
-            start(g, 'HR0', 'HR1', 'HL0', 'HL1', 'MA', 'MB', 'MC', *LSE_TO)
+            start(g, 'HR0', 'HR1', 'HL0', 'HL1', 'S1', 'S2', 'S3', 'S4', 'S5', 'MB', 'MC', 'MA')
 
         @pl.when(stage(t, 2, 2)[1])
         def _():
@@ -290,11 +301,6 @@
             sums(d)
 
         return carry
-
-    def sums(g):
-        arrived(g, 'HR0', 'HR1', 'HL0', 'HL1', 'MB', 'MC', *LSE_TO)
-        partial_sums(g)
-        start(g, 'AR', 'AL', 'TR', 'TL')
 
     lax.fori_loop(0, G + 2, step, 0)
 
@@ -319,7 +325,6 @@
         def _():
             sent(g - 1)
 
-        arrived(g, 'MA', 'AR', 'AL', 'TR', 'TL', 'DR0', 'DR1', 'DL0', 'DL1')
         final(g)
         return carry
 
@@ -349,11 +354,17 @@
                 vmem((G, H, heads, 2 * wd), BF16),
                 vmem((2 * SC, wd, sl), BF16),
                 vmem((G, SC, heads, lat), BF16),
-                vmem((6, G, SC, heads), F32),
-                vmem((2, G, H, heads), F32),
-                vmem((2, G, H, heads), F32),
-                vmem((128, heads), F32),
-                vmem((heads, 128), F32),
+                vmem((SC, heads, 128), F32),
+                vmem((G, 2, 128), F32),
+                vmem((G, 2, 128), F32),
+                vmem((2, G, 1, 128), F32),
+                vmem((2, G, 1, 128), F32),
+                vmem((2, G, 1, 128), F32),
+                vmem((G, 1, 128), F32),
+                vmem((G, 1, 128), F32),
+                vmem((G, 1, 128), F32),
+                vmem((128, 128), F32),
+                vmem((128, 128), F32),
                 vmem((G, SC, hl, lat), BF16),
                 vmem((G, H, hl, lat), BF16),
                 vmem((G, H, hl, lat), BF16),

time: 64.3 us -> 63.6 us (0.989)
  Pallas kernels: 63.4 us -> 62.7 us
    pallas_call x1, Pallas kernels: 63.4 us -> 62.7 us  [local(): pl.pallas_call(functools.partial(kernel, n), out_shape=vmem((G, SC, hl, l...]
where the time goes in v4:
time: 63.6 us; the launch traced here: 63.5 us
  Pallas kernels  62.7 us (99%)
  local copies, waits for them, and re-layouts  0.8 us (1%)
    pallas_call x1, Pallas kernels, local(): pl.pallas_call(functools.partial(kernel, n), out_shape=vmem((G, SC, hl, l...  62.7 us

profile of v4, /device:TPU:88, one launch (start us, length us, event | category | flops | bytes accessed | tf_op | source)
XLA Modules:
  0.0 63.5 jit_solution(15224474037580350138)
XLA Ops:
  0.0 62.7 %shard_map.37 = bf16[8,4,16,512]{3,2,1,0:T(8,128)(2,1)S(1)} custom-call(s32[32]{0:T(128)} %len_hbm.1, bf16[8,4,16,576]{3,2,1,0:T(8,128)(2,1)} %bitcast.7, bf16[8,4,576,1024]{3,2,1,0:T(8,128)(2,1)} %bitcast.6), custom_call_target="tpu_custom_call" | custom-call | tf_op jit(solution)/shard_map/pallas_call | solution.py:346
  62.7 0.8 %copy.5 = bf16[32,16,512]{2,1,0:T(8,128)(2,1)} copy(bf16[32,16,512]{2,1,0:T(8,128)(2,1)S(1)} %bitcast.5) | data formatting | bytes 1048576

commit v5 on v4

--- a/solution.py
+++ b/solution.py
@@ -21,9 +21,16 @@
 
 ROWS = ((1, -1), (0, 0), (2, 1), (-1, 2))
 
-KINDS = ('QR', 'QL', 'FR', 'FL', 'ML', 'MR', 'MO', 'QM', 'S1', 'S2', 'S3', 'S4', 'S5', 'TR', 'TL',
-         'MA', 'MB', 'MC', 'HR0', 'HR1', 'HL0', 'HL1', 'DR0', 'DR1', 'DL0', 'DL1', 'AR', 'AL')
-SEM = {k: i for i, k in enumerate(KINDS)}
+ARRIVE = (('QR', 'QL'), ('FR', 'FL'), ('QM', 'ML', 'MR', 'MO'), ('S1', 'S2', 'S3', 'S4', 'S5'),
+          ('HR0', 'HR1', 'HL0', 'HL1', 'MB', 'MC'), ('TR', 'TL'),
+          ('MA', 'DR0', 'DR1', 'DL0', 'DL1', 'AR', 'AL'))
+NEAR, FAR, QUERIES, LSE, HOPS, SUM_LSE, LAST = range(len(ARRIVE))
+LEAVE = (('QR', 'QL', 'FR', 'FL', 'QM', 'ML', 'MR', 'MO'),
+         ('HR0', 'HR1', 'HL0', 'HL1', 'MA', 'MB', 'MC', 'DR0', 'DR1', 'DL0', 'DL1', 'AR', 'AL'),
+         ('S1', 'S2', 'S3', 'S4', 'S5', 'TR', 'TL'))
+ARRIVE_SEM = {k: c for c, ks in enumerate(ARRIVE) for k in ks}
+LEAVE_SEM = {k: c for c, ks in enumerate(LEAVE) for k in ks}
+
 
 def kernel(n, len_hbm, q_hbm, c_hbm, out_v,
            len_ref, q_st, q_v, c_v, o_v, lse_c, z_own, z_mate, y_s, y_l, y_r, t_s, t_l, t_r, wrow, wt, m_a, m_b, m_c, h_p, h_n, d_p, d_n, a_p, a_n, r_p, r_n,
@@ -118,18 +125,29 @@
             src, dst, to = a_p.at[g], r_p.at[g], right
         else:
             src, dst, to = a_n.at[g], r_n.at[g], left
-        i = SEM[kind]
         return pltpu.make_async_remote_copy(
-            src_ref=src, dst_ref=dst, send_sem=send.at[i, g], recv_sem=recv.at[i, g],
+            src_ref=src, dst_ref=dst, send_sem=send.at[LEAVE_SEM[kind], g], recv_sem=recv.at[ARRIVE_SEM[kind], g],
             device_id={'dcp': to}, device_id_type=pl.DeviceIdType.MESH)
 
     def start(g, *kinds):
         for k in kinds:
             msg(k, g).start()
 
-    def arrived(g, *kinds):
-        for k in kinds:
-            msg(k, g).wait_recv()
+    arrive_bytes = (q_v.at[0, pairs, 0:2 * hl], q_v.at[0, pairs, 0:hl], q_v.at[0, pairs, 0:4 * hl], z_own.at[0:3],
+                    o_v.at[0, 0:3, 0:4 * hl], z_own.at[0], o_v.at[0, both, 0:5 * hl])
+    leave_bytes = (q_v.at[0, pairs, 0:7 * hl], o_v.at[0], z_own.at[0:4])
+
+    def pending(ref, g, c):
+        return pltpu.make_async_remote_copy(
+            src_ref=ref, dst_ref=ref, send_sem=send.at[c % len(LEAVE), g], recv_sem=recv.at[c, g],
+            device_id={'dcp': mate}, device_id_type=pl.DeviceIdType.MESH)
+
+    def arrived(g, c):
+        pending(arrive_bytes[c], g, c).wait_recv()
+
+    def sent(g):
+        for c, ref in enumerate(leave_bytes):
+            pending(ref, g, c).wait_send()
 
     def load(g, i):
         slot = lax.rem(g, 2) * SC + i
@@ -228,10 +246,10 @@
         return w[:, k:k + 1] * o.astype(F32)
 
     def sums(g):
-        arrived(g, 'S1', 'S2', 'S3', 'S4', 'S5')
+        arrived(g, LSE)
         t_s[g] = softmax([z_own[g, 0:1], z_mate[g, 0:1]] + [jnp.where(early, y_l[k, g], y_r[k, g]) for k in range(2)])
         start(g, 'TR', 'TL')
-        arrived(g, 'HR0', 'HR1', 'HL0', 'HL1', 'MB', 'MC')
+        arrived(g, HOPS)
         for i0, d, m, h, a in ((0, right, m_b, h_p, a_p), (H, left, m_c, h_n, a_n)):
             for j in range(H):
                 i = i0 + j
@@ -240,10 +258,10 @@
         start(g, 'AR', 'AL')
 
     def final(g):
-        arrived(g, 'MA', 'TR', 'TL')
+        arrived(g, SUM_LSE)
         softmax([z_own[g, 1:2], z_mate[g, 1:2]] + [jnp.where(early, y_r[k, g], y_l[k, g]) for k in range(2)]
                 + [jnp.where(early, t_l[g], t_r[g])])
-        arrived(g, 'DR0', 'DR1', 'DL0', 'DL1', 'AR', 'AL')
+        arrived(g, LAST)
         for i in range(SC):
             d, r, j = (d_n, r_p, i) if i < H else (d_p, r_n, i - H)
             out_v[g, i] = (weighted(0, i, o_v[g, i, hd(me)]) + weighted(1, i, m_a[g, i])
@@ -259,7 +277,7 @@
 
         @pl.when(on)
         def _():
-            arrived(a, 'QR', 'QL')
+            arrived(a, NEAR)
             start(a, 'FR', 'FL', 'ML', 'MR')
 
         for h in range(QD, G):
@@ -272,7 +290,7 @@
 
         @pl.when(on)
         def _():
-            arrived(b, 'FR', 'FL')
+            arrived(b, FAR)
             start(b, 'MO')
 
         e, on = stage(t, 2 + D2)
@@ -285,7 +303,7 @@
 
         @pl.when(on)
         def _():
-            arrived(g, 'QM', 'ML', 'MR', 'MO')
+            arrived(g, QUERIES)
             attention(g)
             start(g, 'HR0', 'HR1', 'HL0', 'HL1', 'S1', 'S2', 'S3', 'S4', 'S5', 'MB', 'MC', 'MA')
 
@@ -315,10 +333,6 @@
         return carry
 
     lax.fori_loop(G - D1, G, rest, 0)
-
-    def sent(g):
-        for k in KINDS:
-            msg(k, g).wait_send()
 
     def finish(g, carry):
         @pl.when(g >= 1)
@@ -376,8 +390,8 @@
                 vmem((G, H, hl, lat), F32),
                 vmem((G, H, hl, lat), F32),
                 vmem((G, H, hl, lat), F32),
-                pltpu.SemaphoreType.DMA((len(KINDS), G)),
-                pltpu.SemaphoreType.DMA((len(KINDS), G)),
+                pltpu.SemaphoreType.DMA((len(LEAVE), G)),
+                pltpu.SemaphoreType.DMA((len(ARRIVE), G)),
                 pltpu.SemaphoreType.DMA,
                 pltpu.SemaphoreType.DMA((G,)),
                 pltpu.SemaphoreType.DMA((2 * SC,)),

time: 63.6 us -> 60.3 us (0.948)
  Pallas kernels: 62.7 us -> 59.4 us
    pallas_call x1, Pallas kernels: 62.7 us -> 59.4 us  [local(): pl.pallas_call(functools.partial(kernel, n), out_shape=vmem((G, SC, hl, l...]
where the time goes in v5:
time: 60.3 us; the launch traced here: 60.2 us
  Pallas kernels  59.4 us (99%)
  local copies, waits for them, and re-layouts  0.8 us (1%)
    pallas_call x1, Pallas kernels, local(): pl.pallas_call(functools.partial(kernel, n), out_shape=vmem((G, SC, hl, l...  59.4 us

profile of v5, /device:TPU:88, one launch (start us, length us, event | category | flops | bytes accessed | tf_op | source)
XLA Modules:
  0.0 60.2 jit_solution(11117291972253798683)
XLA Ops:
  0.0 59.4 %shard_map.37 = bf16[8,4,16,512]{3,2,1,0:T(8,128)(2,1)S(1)} custom-call(s32[32]{0:T(128)} %len_hbm.1, bf16[8,4,16,576]{3,2,1,0:T(8,128)(2,1)} %bitcast.7, bf16[8,4,576,1024]{3,2,1,0:T(8,128)(2,1)} %bitcast.6), custom_call_target="tpu_custom_call" | custom-call | tf_op jit(solution)/shard_map/pallas_call | solution.py:360
  59.4 0.8 %copy.5 = bf16[32,16,512]{2,1,0:T(8,128)(2,1)} copy(bf16[32,16,512]{2,1,0:T(8,128)(2,1)S(1)} %bitcast.5) | data formatting | bytes 1048576

commit v6 on v5

--- a/solution.py
+++ b/solution.py
@@ -39,7 +39,7 @@
     lat = o_v.shape[3]
     heads = o_v.shape[2]
     hl = heads // n
-    sl = c_v.shape[2]
+    sl = c_v.shape[3]
     nc = n // 2
     me = lax.axis_index('dcp')
     chip = lax.div(me, 2)
@@ -126,7 +126,7 @@
         else:
             src, dst, to = a_n.at[g], r_n.at[g], left
         return pltpu.make_async_remote_copy(
-            src_ref=src, dst_ref=dst, send_sem=send.at[LEAVE_SEM[kind], g], recv_sem=recv.at[ARRIVE_SEM[kind], g],
+            src_ref=src, dst_ref=dst, send_sem=send.at[LEAVE_SEM[kind]], recv_sem=recv.at[ARRIVE_SEM[kind], g],
             device_id={'dcp': to}, device_id_type=pl.DeviceIdType.MESH)
 
     def start(g, *kinds):
@@ -135,45 +135,37 @@
 
     arrive_bytes = (q_v.at[0, pairs, 0:2 * hl], q_v.at[0, pairs, 0:hl], q_v.at[0, pairs, 0:4 * hl], z_own.at[0:3],
                     o_v.at[0, 0:3, 0:4 * hl], z_own.at[0], o_v.at[0, both, 0:5 * hl])
-    leave_bytes = (q_v.at[0, pairs, 0:7 * hl], o_v.at[0], z_own.at[0:4])
+    leave_bytes = (q_v.at[:, :, 0:7 * hl], o_v, lse_c.at[0, 0:8 * G])
 
     def pending(ref, g, c):
         return pltpu.make_async_remote_copy(
-            src_ref=ref, dst_ref=ref, send_sem=send.at[c % len(LEAVE), g], recv_sem=recv.at[c, g],
+            src_ref=ref, dst_ref=ref, send_sem=send.at[c % len(LEAVE)], recv_sem=recv.at[c, g],
             device_id={'dcp': mate}, device_id_type=pl.DeviceIdType.MESH)
 
     def arrived(g, c):
         pending(arrive_bytes[c], g, c).wait_recv()
 
-    def sent(g):
-        for c, ref in enumerate(leave_bytes):
-            pending(ref, g, c).wait_send()
-
-    def load(g, i):
-        slot = lax.rem(g, 2) * SC + i
-        return pltpu.make_async_copy(c_hbm.at[g, i], c_v.at[slot], c_sem.at[slot])
+    def load(g):
+        slot = lax.rem(g, 2)
+        return pltpu.make_async_copy(c_hbm.at[g], c_v.at[slot], c_sem.at[slot])
 
     barrier = pltpu.get_barrier_semaphore()
     for d in (mate, right, right1, left, left1):
         pl.semaphore_signal(barrier, inc=1, device_id={'dcp': d}, device_id_type=pl.DeviceIdType.MESH)
 
-    def fetch(g):
-        return pltpu.make_async_copy(q_hbm.at[g], q_st.at[g], q_sem.at[g])
-
-    def fetch_start(g, carry):
-        fetch(g).start()
-        return carry
-
-    lax.fori_loop(0, G, fetch_start, 0)
+    def fetch(k):
+        part = pl.ds(0, 1) if k == 0 else pl.ds(1, G - 1)
+        return pltpu.make_async_copy(q_hbm.at[part], q_st.at[part], q_sem.at[k])
+
+    fetch(0).start()
+    fetch(1).start()
     lens = pltpu.make_async_copy(len_hbm, len_ref, len_sem)
     lens.start()
     for g in range(min(2, G)):
-        for i in range(SC):
-            load(g, i).start()
+        load(g).start()
     wrow[...] = jnp.zeros_like(wrow)
 
     def pack(g):
-        fetch(g).wait()
         for p in range(H):
             a, b = q_st[g, 2 * p], q_st[g, 2 * p + 1]
             q_v[g, p, hd(me), :lat] = a[:, :lat]
@@ -181,6 +173,8 @@
             q_v[g, p, hd(me), 2 * lat:] = jnp.concatenate([a[:, lat:], b[:, lat:]], axis=1)
 
     for g in range(min(QD, G)):
+        if g < 2:
+            fetch(g).wait()
         pack(g)
         if g == 0:
             pl.semaphore_wait(barrier, 5)
@@ -188,12 +182,11 @@
     lens.wait()
 
     def attention(g):
-        for i in range(SC):
-            load(g, i).wait()
+        load(g).wait()
         pos = me * sl + lax.broadcasted_iota(jnp.int32, (1, sl), 1)
 
         def scores(i):
-            c = c_v.at[lax.rem(g, 2) * SC + i]
+            c = c_v.at[lax.rem(g, 2), i]
             p, r = divmod(i, 2)
             rope = q_v[g, p, :, 2 * lat + r * ROPE:2 * lat + (r + 1) * ROPE]
             return (jnp.dot(q_v[g, p, :, r * lat:(r + 1) * lat], c[:lat], preferred_element_type=F32)
@@ -201,7 +194,7 @@
 
         ahead = scores(0)
         for i in range(SC):
-            c = c_v.at[lax.rem(g, 2) * SC + i]
+            c = c_v.at[lax.rem(g, 2), i]
             s, ahead = ahead, scores(i + 1) if i + 1 < SC else None
             s = jnp.where(pos < len_ref[g * SC + i], s * SCALE, -jnp.inf)
             m = jnp.max(s, axis=1, keepdims=True)
@@ -309,8 +302,7 @@
 
         @pl.when(stage(t, 2, 2)[1])
         def _():
-            for i in range(SC):
-                load(t, i).start()
+            load(t).start()
 
         d, on = stage(t, 2 + D1)
 
@@ -335,15 +327,12 @@
     lax.fori_loop(G - D1, G, rest, 0)
 
     def finish(g, carry):
-        @pl.when(g >= 1)
-        def _():
-            sent(g - 1)
-
         final(g)
         return carry
 
     lax.fori_loop(0, G, finish, 0)
-    sent(G - 1)
+    for c, ref in enumerate(leave_bytes):
+        pending(ref, 0, c).wait_send()
 
 
 def solution(mesh):
@@ -366,7 +355,7 @@
                 pltpu.SMEM((b,), jnp.int32),
                 vmem((G, SC, hl, wd), BF16),
                 vmem((G, H, heads, 2 * wd), BF16),
-                vmem((2 * SC, wd, sl), BF16),
+                vmem((2, SC, wd, sl), BF16),
                 vmem((G, SC, heads, lat), BF16),
                 vmem((SC, heads, 128), F32),
                 vmem((G, 2, 128), F32),
@@ -390,11 +379,11 @@
                 vmem((G, H, hl, lat), F32),
                 vmem((G, H, hl, lat), F32),
                 vmem((G, H, hl, lat), F32),
-                pltpu.SemaphoreType.DMA((len(LEAVE), G)),
+                pltpu.SemaphoreType.DMA((len(LEAVE),)),
                 pltpu.SemaphoreType.DMA((len(ARRIVE), G)),
                 pltpu.SemaphoreType.DMA,
-                pltpu.SemaphoreType.DMA((G,)),
-                pltpu.SemaphoreType.DMA((2 * SC,)),
+                pltpu.SemaphoreType.DMA((2,)),
+                pltpu.SemaphoreType.DMA((2,)),
             ],
             compiler_params=pltpu.CompilerParams(
                 collective_id=0, has_side_effects=True, vmem_limit_bytes=56 * 2 ** 20),

time: 60.3 us -> 60 us (level)
  no operation moved by 1% of the time
where the time goes in v6:
time: 60 us; the launch traced here: 59.9 us
  Pallas kernels  59.1 us (98%)
  local copies, waits for them, and re-layouts  0.8 us (1%)
    pallas_call x1, Pallas kernels, local(): pl.pallas_call(functools.partial(kernel, n), out_shape=vmem((G, SC, hl, l...  59.1 us

profile of v6, /device:TPU:88, one launch (start us, length us, event | category | flops | bytes accessed | tf_op | source)
XLA Modules:
  0.0 59.9 jit_solution(13211014958112314681)
XLA Ops:
  0.0 59.1 %shard_map.37 = bf16[8,4,16,512]{3,2,1,0:T(8,128)(2,1)S(1)} custom-call(s32[32]{0:T(128)} %len_hbm.1, bf16[8,4,16,576]{3,2,1,0:T(8,128)(2,1)} %bitcast.7, bf16[8,4,576,1024]{3,2,1,0:T(8,128)(2,1)} %bitcast.6), custom_call_target="tpu_custom_call" | custom-call | tf_op jit(solution)/shard_map/pallas_call | solution.py:349
  59.1 0.8 %copy.5 = bf16[32,16,512]{2,1,0:T(8,128)(2,1)} copy(bf16[32,16,512]{2,1,0:T(8,128)(2,1)S(1)} %bitcast.5) | data formatting | bytes 1048576

commit v7 on v6

--- a/solution.py
+++ b/solution.py
@@ -243,12 +243,12 @@
         t_s[g] = softmax([z_own[g, 0:1], z_mate[g, 0:1]] + [jnp.where(early, y_l[k, g], y_r[k, g]) for k in range(2)])
         start(g, 'TR', 'TL')
         arrived(g, HOPS)
-        for i0, d, m, h, a in ((0, right, m_b, h_p, a_p), (H, left, m_c, h_n, a_n)):
+        for i0, d, m, h, a, k in ((0, right, m_b, h_p, a_p, 'AR'), (H, left, m_c, h_n, a_n, 'AL')):
             for j in range(H):
                 i = i0 + j
                 a[g, j] = (weighted(0, i, o_v[g, i, hd(d)]) + weighted(1, i, m[g, j])
                            + weighted(2, i, h[0, g, j]) + weighted(3, i, h[1, g, j]))
-        start(g, 'AR', 'AL')
+            start(g, k)
 
     def final(g):
         arrived(g, SUM_LSE)
@@ -280,6 +280,7 @@
                 start(h, 'QR', 'QL', 'QM')
 
         b, on = stage(t, 1)
+        on = on & (t != 2)
 
         @pl.when(on)
         def _():
@@ -299,6 +300,14 @@
             arrived(g, QUERIES)
             attention(g)
             start(g, 'HR0', 'HR1', 'HL0', 'HL1', 'S1', 'S2', 'S3', 'S4', 'S5', 'MB', 'MC', 'MA')
+
+        b, on = stage(t, 1)
+        on = on & (t == 2)
+
+        @pl.when(on)
+        def _():
+            arrived(b, FAR)
+            start(b, 'MO')
 
         @pl.when(stage(t, 2, 2)[1])
         def _():

time: 60 us -> 59.9 us (level)
  no operation moved by 1% of the time
where the time goes in v7:
time: 59.9 us
  Pallas kernels  59 us (98%)
  local copies, waits for them, and re-layouts  0.8 us (1%)
    pallas_call x1, Pallas kernels, local(): pl.pallas_call(functools.partial(kernel, n), out_shape=vmem((G, SC, hl, l...  59 us

profile of v7, /device:TPU:88, one launch (start us, length us, event | category | flops | bytes accessed | tf_op | source)
XLA Modules:
  0.0 59.9 jit_solution(2752371156918072347)
XLA Ops:
  0.0 59.0 %shard_map.37 = bf16[8,4,16,512]{3,2,1,0:T(8,128)(2,1)S(1)} custom-call(s32[32]{0:T(128)} %len_hbm.1, bf16[8,4,16,576]{3,2,1,0:T(8,128)(2,1)} %bitcast.7, bf16[8,4,576,1024]{3,2,1,0:T(8,128)(2,1)} %bitcast.6), custom_call_target="tpu_custom_call" | custom-call | tf_op jit(solution)/shard_map/pallas_call | solution.py:358
  59.1 0.8 %copy.5 = bf16[32,16,512]{2,1,0:T(8,128)(2,1)} copy(bf16[32,16,512]{2,1,0:T(8,128)(2,1)S(1)} %bitcast.5) | data formatting | bytes 1048576
